TPU v7x, 32 devices: a whole 2x2x4 slice. The times are simulated.
32 devices in a mesh: row: 2 (over y), col: 4 (over x, core), band: 4 (over z).
Axes of the slice: x: 2, y: 2, z: 4, core: 2. Of those that a mesh axis runs over, the one named last changes fastest.
Arguments:
- noisy: float32 [224, 32, 4096], P('band', 'row', 'col'), may hold values from -4 to 4
- weight_map: float32 [32, 4096], P('row', 'col'), may hold values from 1.5 to 12
Outputs:
- denoised: float32 [224, 32, 4096], P('band', 'row', 'col')
All inputs are finite; a program needn't handle non-finite values.
Results may differ from a plain program's by a relative error of at most 0.0001.
Values sent between devices are 32-bit elements; how exact they have to be, the bound alone decides.
A program may use at most 64 MiB of HBM per device.

v0:
```python
import functools

import jax
import jax.numpy as jnp
from jax import lax
from jax.experimental import pallas as pl
from jax.experimental.pallas import tpu as pltpu
from jax.sharding import PartitionSpec as P

ITERS = 4
dual_step = 0.35
primal_step = 0.35
KEEP = 1.0 / (1.0 + primal_step)
GAIN = primal_step / (1.0 + primal_step)
STEP = GAIN * dual_step
LANES = 128
MESH = pl.DeviceIdType.MESH


def kernel(n_row, n_col, n_band, x_ref, w_ref, out_ref,
           N, U, W, QX, QY, HU, HD, E, ER, EL, WT, SC, CY, S, SE, R, RE,
           in_sem, out_sem, ys, yr, xs, xr, zs, zr):
    rows, bands, cols = x_ref.shape
    wide = cols + LANES
    groups = bands // 8
    last = rows - 1
    ri = lax.axis_index("row")
    ci = lax.axis_index("col")
    bi = lax.axis_index("band")
    has_up = ri > 0
    has_down = ri < n_row - 1
    has_left = ci > 0
    has_right = ci < n_col - 1

    fetch = pltpu.make_async_copy(x_ref, N.at[:, 0:bands, 0:cols], in_sem)
    fetch.start()

    barrier = pltpu.get_barrier_semaphore()
    for cond, axis, target in ((has_up, "row", ri - 1), (has_down, "row", ri + 1),
                               (has_left, "col", ci - 1), (has_right, "col", ci + 1)):
        @pl.when(cond)
        def _():
            pl.semaphore_signal(barrier, inc=1, device_id={axis: target}, device_id_type=MESH)
    for d in range(1, n_band):
        pl.semaphore_signal(barrier, inc=1, device_id={"band": lax.rem(bi + d, n_band)}, device_id_type=MESH)
    count = (n_band - 1 + has_up.astype(jnp.int32) + has_down.astype(jnp.int32)
             + has_left.astype(jnp.int32) + has_right.astype(jnp.int32))

    def up_copy(i, src, dst):
        return pltpu.make_async_remote_copy(
            src_ref=src, dst_ref=dst, send_sem=ys.at[0, i], recv_sem=yr.at[0, i],
            device_id={"row": ri - 1}, device_id_type=MESH)

    def down_copy(i, src, dst):
        return pltpu.make_async_remote_copy(
            src_ref=src, dst_ref=dst, send_sem=ys.at[1, i], recv_sem=yr.at[1, i],
            device_id={"row": ri + 1}, device_id_type=MESH)

    def y_pair(k, part):
        if k == 0:
            span = pl.ds(0, cols) if part == 0 else pl.ds(cols, LANES)
            i = 0 if part == 0 else ITERS
            return (up_copy(i, N.at[0, :, span], HU.at[0, :, span]),
                    down_copy(i, N.at[last, :, span], HD.at[0, :, span]))
        span = pl.ds(0, bands)
        return (up_copy(k, W.at[0], HU.at[k, span]), down_copy(k, W.at[last], HD.at[k, span]))

    def y_start(k, part=0):
        up, down = y_pair(k, part)

        @pl.when(has_up)
        def _():
            up.start()

        @pl.when(has_down)
        def _():
            down.start()

    def y_recv(k, part=0):
        up, down = y_pair(k, part)

        @pl.when(has_down)
        def _():
            up.wait_recv()

        @pl.when(has_up)
        def _():
            down.wait_recv()

    def y_sent(k, part=0):
        up, down = y_pair(k, part)

        @pl.when(has_up)
        def _():
            up.wait_send()

        @pl.when(has_down)
        def _():
            down.wait_send()

    def z_copy(k, d, part):
        if part < 2:
            half = pl.ds(part * 8, 8)
            src, dst = S.at[k, half], R.at[k, d - 1, half]
        else:
            src, dst = SE.at[k], RE.at[k, d - 1]
        return pltpu.make_async_remote_copy(
            src_ref=src, dst_ref=dst, send_sem=zs.at[k, d - 1, part], recv_sem=zr.at[k, d - 1, part],
            device_id={"band": lax.rem(bi + d, n_band)}, device_id_type=MESH)

    def z_start(k, part):
        for d in range(1, n_band):
            z_copy(k, d, part).start()

    def total(k, part):
        for d in range(1, n_band):
            z_copy(k, d, part).wait_recv()
        if part < 2:
            half = pl.ds(part * 8, 8)
            acc = S[k, half]
            for d in range(1, n_band):
                acc = acc + R[k, d - 1, half]
            return acc
        acc = SE[k]
        for d in range(1, n_band):
            acc = acc + RE[k, d - 1]
        return acc

    def scale_of(weight, squares):
        return weight / jnp.maximum(weight, jnp.sqrt(1.0 + squares * (1.0 / (GAIN * GAIN))))

    def sync(k):
        for part in range(2):
            half = pl.ds(part * 8, 8)
            SC[half] = scale_of(WT[half], total(k, part))
        edge = total(k, 2)
        SC[pl.ds(last, 1)] = scale_of(WT[pl.ds(last, 1)], edge[0:1])
        SC[pl.ds(rows, 1)] = scale_of(WT[pl.ds(rows, 1)], edge[1:2])

    def left_of(v):
        return pltpu.roll(v, 1, 1)

    def right_of(v):
        return pltpu.roll(v, wide - 1, 1)

    pl.semaphore_wait(barrier, count)

    lane = lax.broadcasted_iota(jnp.int32, (1, wide), 1)
    column = ci * cols + jnp.where(lane < cols + LANES // 2, lane, lane - wide)
    CY[...] = jnp.where((column >= 0) & (column < n_col * cols - 1), STEP, 0.0)

    def put_weight(r, _):
        N[r, pl.ds(bands, 8), 0:cols] = jnp.broadcast_to(w_ref[pl.ds(r, 1), :], (8, cols))
        return 0
    lax.fori_loop(0, rows, put_weight, 0)
    S[:, pl.ds(8, 8), :] = jnp.zeros((ITERS, 8, wide), jnp.float32)

    @pl.when(jnp.logical_not(has_down))
    def _():
        HU[...] = jnp.zeros_like(HU)

    @pl.when(jnp.logical_not(has_up))
    def _():
        HD[...] = jnp.zeros_like(HD)

    @pl.when(jnp.logical_not(has_right))
    def _():
        ER[...] = jnp.zeros_like(ER)

    @pl.when(jnp.logical_not(has_left))
    def _():
        EL[...] = jnp.zeros_like(EL)

    fetch.wait()
    y_start(0, 0)

    pitch = 2 * ITERS
    spot = lax.broadcasted_iota(jnp.int32, (8, LANES), 1)

    def pack(g, _):
        span = pl.ds(pl.multiple_of(g * 8, 8), 8)
        acc = jnp.zeros((8, LANES), jnp.float32)
        for r in range(rows):
            at = r * pitch
            head = pltpu.roll(N[r, span, 0:LANES], at % LANES, 1)
            tail = pltpu.roll(N[r, span, cols - LANES:cols], (at + pitch) % LANES, 1)
            acc = jnp.where((spot >= at) & (spot < at + ITERS), head, acc)
            acc = jnp.where((spot >= at + ITERS) & (spot < at + pitch), tail, acc)
        E[span] = acc
        return 0
    lax.fori_loop(0, groups + 1, pack, 0)

    to_left = pltpu.make_async_remote_copy(
        src_ref=E, dst_ref=ER, send_sem=xs.at[0], recv_sem=xr.at[0],
        device_id={"col": ci - 1}, device_id_type=MESH)
    to_right = pltpu.make_async_remote_copy(
        src_ref=E, dst_ref=EL, send_sem=xs.at[1], recv_sem=xr.at[1],
        device_id={"col": ci + 1}, device_id_type=MESH)

    @pl.when(has_left)
    def _():
        to_left.start()

    @pl.when(has_right)
    def _():
        to_right.start()

    @pl.when(has_right)
    def _():
        to_left.wait_recv()

    @pl.when(has_left)
    def _():
        to_right.wait_recv()

    def unpack(g, _):
        span = pl.ds(pl.multiple_of(g * 8, 8), 8)
        from_right, from_left = ER[span], EL[span]
        for r in range(rows):
            at = r * pitch
            head = pltpu.roll(from_right, (LANES - at) % LANES, 1)
            tail = pltpu.roll(from_left, (LANES - at - pitch) % LANES, 1)
            N[r, span, cols:wide] = jnp.where(spot < LANES // 2, head, tail)
        return 0
    lax.fori_loop(0, groups + 1, unpack, 0)
    y_start(0, 1)

    def put_wt(r, _):
        WT[pl.ds(r, 1)] = N[r, pl.ds(bands, 1), :]
        return 0
    lax.fori_loop(0, rows, put_wt, 0)

    def span_of(g):
        return pl.ds(g * 8, 8)

    def group_sum(acc):
        return jnp.sum(acc, axis=0, keepdims=True)

    def dual_row(r, own, nxt, cx, first):
        acc = jnp.zeros((8, wide), jnp.float32)
        cy = CY[...]
        sc = None if first else SC[pl.ds(r, 1)]
        for g in range(groups):
            wu, w = own(g), nxt(g)
            qx = cx * (w - wu)
            qy = cy * (right_of(wu) - wu)
            if not first:
                qx = sc * QX[r, span_of(g)] + qx
                qy = sc * QY[r, span_of(g)] + qy
            QX[r, span_of(g)] = qx
            QY[r, span_of(g)] = qy
            acc = acc + (qx * qx + qy * qy)
        return group_sum(acc)

    cx_last = jnp.where(has_down, STEP, 0.0)
    cx_above = jnp.where(has_up, STEP, 0.0)

    def edges(k, field):
        y_recv(k, 0)
        if k == 0:
            y_recv(0, 1)
            WT[pl.ds(rows, 1)] = HD[0, pl.ds(bands, 1), :]
        SE[k, pl.ds(0, 1)] = dual_row(last, lambda g: field[last, span_of(g)],
                                      lambda g: HU[k, span_of(g)], cx_last, k == 0)
        SE[k, pl.ds(1, 1)] = dual_row(rows, lambda g: HD[k, span_of(g)],
                                      lambda g: field[0, span_of(g)], cx_above, k == 0)
        z_start(k, 2)

    def primal_group(r, above, g, first):
        sc, su = SC[pl.ds(r, 1)], SC[pl.ds(above, 1)]
        pu = su * QX[above, span_of(g)]
        px = sc * QX[r, span_of(g)]
        py = sc * QY[r, span_of(g)]
        div = (px - pu) + (py - left_of(py))
        given = N[r, span_of(g)]
        if first:
            u = given
            new = given + div
        else:
            u = U[r, span_of(g)]
            new = KEEP * u + (GAIN * given + div)
        U[r, span_of(g)] = new
        return pu, new, u

    def primal_row(r, above, first):
        for g in range(groups):
            _, new, u = primal_group(r, above, g, first)
            W[r, span_of(g)] = 2.0 * new - u

    def start_row(r, _):
        S[0, pl.ds(r, 1)] = dual_row(r, lambda g: N[r, span_of(g)], lambda g: N[r + 1, span_of(g)], STEP, True)
        return 0
    lax.fori_loop(0, 8, start_row, 0)
    z_start(0, 0)
    lax.fori_loop(8, last, start_row, 0)
    z_start(0, 1)
    edges(0, N)
    sync(0)

    for k in range(1, ITERS):
        first = k == 1
        if k > 1:
            y_sent(k - 1)
        primal_row(0, rows, first)
        primal_row(last, last - 1, first)
        y_start(k)

        def both(r, _, first=first, k=k):
            acc = jnp.zeros((8, wide), jnp.float32)
            cy = CY[...]
            su = SC[pl.ds(r - 1, 1)]
            for g in range(groups):
                pu, new, u = primal_group(r, r - 1, g, first)
                w = 2.0 * new - u
                W[r, span_of(g)] = w
                wu = W[r - 1, span_of(g)]
                qx = pu + STEP * (w - wu)
                qy = su * QY[r - 1, span_of(g)] + cy * (right_of(wu) - wu)
                QX[r - 1, span_of(g)] = qx
                QY[r - 1, span_of(g)] = qy
                acc = acc + (qx * qx + qy * qy)
            S[k, pl.ds(r - 1, 1)] = group_sum(acc)
            return 0
        lax.fori_loop(1, 9, both, 0)
        z_start(k, 0)
        lax.fori_loop(9, last, both, 0)
        S[k, pl.ds(last - 1, 1)] = dual_row(last - 1, lambda g: W[last - 1, span_of(g)],
                                            lambda g: W[last, span_of(g)], STEP, False)
        z_start(k, 1)
        edges(k, W)
        sync(k)

    def finish(r, above):
        for g in range(groups):
            primal_group(r, above, g, False)
        pltpu.make_async_copy(U.at[r, :, 0:cols], out_ref.at[r], out_sem.at[r]).start()

    finish(0, rows)

    def finish_row(r, _):
        finish(r, r - 1)
        return 0
    lax.fori_loop(1, rows, finish_row, 0)

    y_sent(0, 0)
    y_sent(0, 1)
    y_sent(ITERS - 1)

    @pl.when(has_left)
    def _():
        to_left.wait_send()

    @pl.when(has_right)
    def _():
        to_right.wait_send()
    for k in range(ITERS):
        for d in range(1, n_band):
            for part in range(3):
                z_copy(k, d, part).wait_send()

    def drain(r, _):
        pltpu.make_async_copy(U.at[r, :, 0:cols], out_ref.at[r], out_sem.at[r]).wait()
        return 0
    lax.fori_loop(0, rows, drain, 0)


def local(n_row, n_col, n_band, noisy, weight_map):
    bands, rows, cols = noisy.shape
    padded = -(-bands // 8) * 8
    x = jnp.transpose(noisy, (1, 0, 2))
    if padded != bands:
        x = jnp.pad(x, ((0, 0), (0, padded - bands), (0, 0)))
    wide = cols + LANES
    f32 = jnp.float32
    peers = n_band - 1
    dma = pltpu.SemaphoreType.DMA
    out = pl.pallas_call(
        functools.partial(kernel, n_row, n_col, n_band),
        out_shape=jax.ShapeDtypeStruct((rows, padded, cols), f32),
        in_specs=[pl.BlockSpec(memory_space=pl.ANY), pl.BlockSpec(memory_space=pltpu.VMEM)],
        out_specs=pl.BlockSpec(memory_space=pl.ANY),
        scratch_shapes=[
            pltpu.VMEM((rows, padded + 8, wide), f32),
            pltpu.VMEM((rows, padded, wide), f32),
            pltpu.VMEM((rows, padded, wide), f32),
            pltpu.VMEM((rows + 1, padded, wide), f32),
            pltpu.VMEM((rows + 1, padded, wide), f32),
            pltpu.VMEM((ITERS, padded + 8, wide), f32),
            pltpu.VMEM((ITERS, padded + 8, wide), f32),
            pltpu.VMEM((padded + 8, LANES), f32),
            pltpu.VMEM((padded + 8, LANES), f32),
            pltpu.VMEM((padded + 8, LANES), f32),
            pltpu.VMEM((rows + 8, wide), f32),
            pltpu.VMEM((rows + 8, wide), f32),
            pltpu.VMEM((1, wide), f32),
            pltpu.VMEM((ITERS, rows, wide), f32),
            pltpu.VMEM((ITERS, 2, wide), f32),
            pltpu.VMEM((ITERS, peers, rows, wide), f32),
            pltpu.VMEM((ITERS, peers, 2, wide), f32),
            dma, dma((rows,)),
            dma((2, ITERS + 1)), dma((2, ITERS + 1)),
            dma((2,)), dma((2,)),
            dma((ITERS, peers, 3)), dma((ITERS, peers, 3)),
        ],
        compiler_params=pltpu.CompilerParams(
            collective_id=0, has_side_effects=True, vmem_limit_bytes=48 * 1024 * 1024),
    )(x, weight_map)
    return jnp.transpose(out[:, :bands], (1, 0, 2))


def solution(mesh):
    placed = (P("band", "row", "col"), P("row", "col"))
    sizes = dict(mesh.shape)
    body = functools.partial(local, sizes["row"], sizes["col"], sizes["band"])
    return jax.shard_map(
        body, mesh=mesh, in_specs=placed, out_specs=P("band", "row", "col"), check_vma=False
    )
```

profile of v0, /device:TPU:0, one launch (start us, length us, event | category | flops | bytes accessed | tf_op | source)
XLA Modules:
  0.0 102.0 jit_solution(14739498923113102172)
XLA Ops:
  0.0 0.0 copy-start
  0.0 6.0 %copy.6 = f32[56,16,1024]{2,0,1:T(8,128)} copy(f32[56,16,1024]{2,1,0:T(8,128)} %param.2) | data formatting | bytes 7340032 | tf_op args[0]
  6.0 0.0 copy-done
  6.0 92.0 %shard_map.28 = f32[16,56,1024]{2,1,0:T(8,128)S(1)} custom-call(f32[16,56,1024]{2,1,0:T(8,128)} %bitcast.5, f32[16,1024]{1,0:T(8,128)S(1)} %copy-done), custom_call_target="tpu_custom_call" | custom-call | tf_op jit(solution)/shard_map/pallas_call | solution.py:377
  98.0 4.0 %copy.4 = f32[56,16,1024]{2,1,0:T(8,128)} copy(f32[56,16,1024]{2,0,1:T(8,128)S(1)} %bitcast.4) | data formatting | bytes 7340032 | tf_op jit(solution)/shard_map/transpose | solution.py:408
Async XLA Ops:
  0.0 6.0 %copy-start = (f32[16,1024]{1,0:T(8,128)S(1)}, f32[16,1024]{1,0:T(8,128)}, u32[]{:S(2)}) copy-start(f32[16,1024]{1,0:T(8,128)} %w_ref.1) | copy-start | bytes 196612
where the time goes:
time: 102 us
  Pallas kernels  92 us (90%)
  local copies, waits for them, and re-layouts  10 us (10%)
    pallas_call x1, Pallas kernels, local(): pl.pallas_call(functools.partial(kernel, n_row, n_col, n_band), out_shape...  92 us
    unnamed x3, local copies, waits for them, and re-layouts  6.04 us
    transpose x1, local copies, waits for them, and re-layouts, local(): return jnp.transpose(out[:, :bands], (1, 0, 2))  3.96 us

commit v1 on v0

--- a/solution.py
+++ b/solution.py
@@ -19,6 +19,7 @@
 
 def kernel(n_row, n_col, n_band, x_ref, w_ref, out_ref,
            N, U, W, QX, QY, HU, HD, E, ER, EL, WT, SC, CY, S, SE, R, RE,
+           LA, LB, FA, FB, MA, MB,
            in_sem, out_sem, ys, yr, xs, xr, zs, zr):
     rows, bands, cols = x_ref.shape
     wide = cols + LANES
@@ -129,19 +130,58 @@
     def scale_of(weight, squares):
         return weight / jnp.maximum(weight, jnp.sqrt(1.0 + squares * (1.0 / (GAIN * GAIN))))
 
+    def put_scale(r, v):
+        SC[r] = jnp.broadcast_to(v, (8, wide))
+
     def sync(k):
         for part in range(2):
             half = pl.ds(part * 8, 8)
-            SC[half] = scale_of(WT[half], total(k, part))
+            values = scale_of(WT[half], total(k, part))
+            for i in range(8):
+                if part * 8 + i < last:
+                    put_scale(part * 8 + i, values[i:i + 1])
         edge = total(k, 2)
-        SC[pl.ds(last, 1)] = scale_of(WT[pl.ds(last, 1)], edge[0:1])
-        SC[pl.ds(rows, 1)] = scale_of(WT[pl.ds(rows, 1)], edge[1:2])
-
-    def left_of(v):
-        return pltpu.roll(v, 1, 1)
-
-    def right_of(v):
-        return pltpu.roll(v, wide - 1, 1)
+        put_scale(last, scale_of(WT[pl.ds(last, 1)], edge[0:1]))
+        put_scale(rows, scale_of(WT[pl.ds(rows, 1)], edge[1:2]))
+
+    tiles = wide // LANES
+    pitch_m = LA.shape[0] // tiles
+
+    def tile(j):
+        return pl.ds((j % tiles) * LANES, LANES)
+
+    def part_of(F, j):
+        at = (j % tiles) * pitch_m
+        return F.at[pl.ds(at, bands), 0:LANES], F.at[pl.ds(at, bands), LANES:2 * LANES]
+
+    def difference(L, F, M, load, neighbour):
+        for j in range(tiles):
+            v = load(j)
+            high = v.astype(jnp.bfloat16)
+            low = (v - high.astype(jnp.float32)).astype(jnp.bfloat16)
+            L[pl.ds(j * pitch_m, bands), 0:LANES] = high
+            L[pl.ds(j * pitch_m, bands), LANES:2 * LANES] = low
+        F[...] = jnp.dot(L[...], M[...], preferred_element_type=jnp.float32)
+        return lambda j: part_of(F, j)[0][...] + part_of(F, j + neighbour)[1][...]
+
+    def right_diff(load):
+        return difference(LA, FA, MA, load, 1)
+
+    def left_diff(load):
+        return difference(LB, FB, MB, load, -1)
+
+    at_in = lax.broadcasted_iota(jnp.int32, (2 * LANES, 2 * LANES), 0) % LANES
+    at_out = lax.broadcasted_iota(jnp.int32, (2 * LANES, 2 * LANES), 1)
+
+    def plus(cond):
+        return jnp.where(cond, 1.0, 0.0)
+    inside = at_out < LANES
+    MA[...] = (plus(inside & (at_in == at_out + 1)) - plus(inside & (at_in == at_out))
+               + plus((at_out == 2 * LANES - 1) & (at_in == 0))).astype(jnp.bfloat16)
+    MB[...] = (plus(inside & (at_in == at_out)) - plus(inside & (at_in == at_out - 1))
+               - plus((at_out == LANES) & (at_in == LANES - 1))).astype(jnp.bfloat16)
+    LA[...] = jnp.zeros_like(LA)
+    LB[...] = jnp.zeros_like(LB)
 
     pl.semaphore_wait(barrier, count)
 
@@ -230,27 +270,33 @@
         return 0
     lax.fori_loop(0, rows, put_wt, 0)
 
-    def span_of(g):
-        return pl.ds(g * 8, 8)
-
-    def group_sum(acc):
-        return jnp.sum(acc, axis=0, keepdims=True)
-
-    def dual_row(r, own, nxt, cx, first):
-        acc = jnp.zeros((8, wide), jnp.float32)
-        cy = CY[...]
-        sc = None if first else SC[pl.ds(r, 1)]
-        for g in range(groups):
-            wu, w = own(g), nxt(g)
-            qx = cx * (w - wu)
-            qy = cy * (right_of(wu) - wu)
+    full = pl.ds(0, bands)
+
+    def dual_row(r, own, nxt, cx, first, put):
+        grad = right_diff(own)
+        sums = []
+        for j in range(tiles):
+            t = tile(j)
+            qx = cx * (nxt(j) - own(j))
+            qy = CY[:, t] * grad(j)
             if not first:
-                qx = sc * QX[r, span_of(g)] + qx
-                qy = sc * QY[r, span_of(g)] + qy
-            QX[r, span_of(g)] = qx
-            QY[r, span_of(g)] = qy
-            acc = acc + (qx * qx + qy * qy)
-        return group_sum(acc)
+                sc = SC[r, 0:1, t]
+                qx = sc * QX[r, :, t] + qx
+                qy = sc * QY[r, :, t] + qy
+            QX[r, :, t] = qx
+            QY[r, :, t] = qy
+            sums.append(jnp.sum(qx * qx + qy * qy, axis=0, keepdims=True))
+        put(jnp.concatenate(sums, axis=1))
+
+    def put_main(k, r):
+        def put(v):
+            S[k, pl.ds(r, 1)] = v
+        return put
+
+    def put_edge(k, i):
+        def put(v):
+            SE[k, pl.ds(i, 1)] = v
+        return put
 
     cx_last = jnp.where(has_down, STEP, 0.0)
     cx_above = jnp.where(has_up, STEP, 0.0)
@@ -260,35 +306,38 @@
         if k == 0:
             y_recv(0, 1)
             WT[pl.ds(rows, 1)] = HD[0, pl.ds(bands, 1), :]
-        SE[k, pl.ds(0, 1)] = dual_row(last, lambda g: field[last, span_of(g)],
-                                      lambda g: HU[k, span_of(g)], cx_last, k == 0)
-        SE[k, pl.ds(1, 1)] = dual_row(rows, lambda g: HD[k, span_of(g)],
-                                      lambda g: field[0, span_of(g)], cx_above, k == 0)
+        dual_row(last, lambda j: field[last, full, tile(j)], lambda j: HU[k, full, tile(j)],
+                 cx_last, k == 0, put_edge(k, 0))
+        dual_row(rows, lambda j: HD[k, full, tile(j)], lambda j: field[0, full, tile(j)],
+                 cx_above, k == 0, put_edge(k, 1))
         z_start(k, 2)
 
-    def primal_group(r, above, g, first):
-        sc, su = SC[pl.ds(r, 1)], SC[pl.ds(above, 1)]
-        pu = su * QX[above, span_of(g)]
-        px = sc * QX[r, span_of(g)]
-        py = sc * QY[r, span_of(g)]
-        div = (px - pu) + (py - left_of(py))
-        given = N[r, span_of(g)]
+    def scaled_y(r):
+        return left_diff(lambda j: SC[r, 0:1, tile(j)] * QY[r, :, tile(j)])
+
+    def primal_tile(r, above, j, first, div_y):
+        t = tile(j)
+        pu = SC[above, 0:1, t] * QX[above, :, t]
+        px = SC[r, 0:1, t] * QX[r, :, t]
+        div = (px - pu) + div_y(j)
+        given = N[r, full, t]
         if first:
             u = given
             new = given + div
         else:
-            u = U[r, span_of(g)]
+            u = U[r, :, t]
             new = KEEP * u + (GAIN * given + div)
-        U[r, span_of(g)] = new
+        U[r, :, t] = new
         return pu, new, u
 
     def primal_row(r, above, first):
-        for g in range(groups):
-            _, new, u = primal_group(r, above, g, first)
-            W[r, span_of(g)] = 2.0 * new - u
+        div_y = scaled_y(r)
+        for j in range(tiles):
+            _, new, u = primal_tile(r, above, j, first, div_y)
+            W[r, :, tile(j)] = 2.0 * new - u
 
     def start_row(r, _):
-        S[0, pl.ds(r, 1)] = dual_row(r, lambda g: N[r, span_of(g)], lambda g: N[r + 1, span_of(g)], STEP, True)
+        dual_row(r, lambda j: N[r, full, tile(j)], lambda j: N[r + 1, full, tile(j)], STEP, True, put_main(0, r))
         return 0
     lax.fori_loop(0, 8, start_row, 0)
     z_start(0, 0)
@@ -306,33 +355,34 @@
         y_start(k)
 
         def both(r, _, first=first, k=k):
-            acc = jnp.zeros((8, wide), jnp.float32)
-            cy = CY[...]
-            su = SC[pl.ds(r - 1, 1)]
-            for g in range(groups):
-                pu, new, u = primal_group(r, r - 1, g, first)
+            div_y = scaled_y(r)
+            grad = right_diff(lambda j: W[r - 1, :, tile(j)])
+            sums = []
+            for j in range(tiles):
+                t = tile(j)
+                pu, new, u = primal_tile(r, r - 1, j, first, div_y)
                 w = 2.0 * new - u
-                W[r, span_of(g)] = w
-                wu = W[r - 1, span_of(g)]
-                qx = pu + STEP * (w - wu)
-                qy = su * QY[r - 1, span_of(g)] + cy * (right_of(wu) - wu)
-                QX[r - 1, span_of(g)] = qx
-                QY[r - 1, span_of(g)] = qy
-                acc = acc + (qx * qx + qy * qy)
-            S[k, pl.ds(r - 1, 1)] = group_sum(acc)
+                W[r, :, t] = w
+                qx = pu + STEP * (w - W[r - 1, :, t])
+                qy = SC[r - 1, 0:1, t] * QY[r - 1, :, t] + CY[:, t] * grad(j)
+                QX[r - 1, :, t] = qx
+                QY[r - 1, :, t] = qy
+                sums.append(jnp.sum(qx * qx + qy * qy, axis=0, keepdims=True))
+            S[k, pl.ds(r - 1, 1)] = jnp.concatenate(sums, axis=1)
             return 0
         lax.fori_loop(1, 9, both, 0)
         z_start(k, 0)
         lax.fori_loop(9, last, both, 0)
-        S[k, pl.ds(last - 1, 1)] = dual_row(last - 1, lambda g: W[last - 1, span_of(g)],
-                                            lambda g: W[last, span_of(g)], STEP, False)
+        dual_row(last - 1, lambda j: W[last - 1, :, tile(j)], lambda j: W[last, :, tile(j)],
+                 STEP, False, put_main(k, last - 1))
         z_start(k, 1)
         edges(k, W)
         sync(k)
 
     def finish(r, above):
-        for g in range(groups):
-            primal_group(r, above, g, False)
+        div_y = scaled_y(r)
+        for j in range(tiles):
+            primal_tile(r, above, j, False, div_y)
         pltpu.make_async_copy(U.at[r, :, 0:cols], out_ref.at[r], out_sem.at[r]).start()
 
     finish(0, rows)
@@ -371,7 +421,8 @@
     if padded != bands:
         x = jnp.pad(x, ((0, 0), (0, padded - bands), (0, 0)))
     wide = cols + LANES
-    f32 = jnp.float32
+    f32, bf16 = jnp.float32, jnp.bfloat16
+    depth = wide // LANES * (-(-padded // 16) * 16)
     peers = n_band - 1
     dma = pltpu.SemaphoreType.DMA
     out = pl.pallas_call(
@@ -391,12 +442,18 @@
             pltpu.VMEM((padded + 8, LANES), f32),
             pltpu.VMEM((padded + 8, LANES), f32),
             pltpu.VMEM((rows + 8, wide), f32),
-            pltpu.VMEM((rows + 8, wide), f32),
+            pltpu.VMEM((rows + 1, 8, wide), f32),
             pltpu.VMEM((1, wide), f32),
             pltpu.VMEM((ITERS, rows, wide), f32),
             pltpu.VMEM((ITERS, 2, wide), f32),
             pltpu.VMEM((ITERS, peers, rows, wide), f32),
             pltpu.VMEM((ITERS, peers, 2, wide), f32),
+            pltpu.VMEM((depth, 2 * LANES), bf16),
+            pltpu.VMEM((depth, 2 * LANES), bf16),
+            pltpu.VMEM((depth, 2 * LANES), f32),
+            pltpu.VMEM((depth, 2 * LANES), f32),
+            pltpu.VMEM((2 * LANES, 2 * LANES), bf16),
+            pltpu.VMEM((2 * LANES, 2 * LANES), bf16),
             dma, dma((rows,)),
             dma((2, ITERS + 1)), dma((2, ITERS + 1)),
             dma((2,)), dma((2,)),

time: 102 us -> 77.4 us (0.76)
  Pallas kernels: 92 us -> 67.3 us
    pallas_call x1, Pallas kernels: 92 us -> 67.3 us  [local(): pl.pallas_call(functools.partial(kernel, n_row, n_col, n_band), out_shape...]
where the time goes in v1:
time: 77.4 us; the launch traced here: 77.3 us
  Pallas kernels  67.3 us (87%)
  local copies, waits for them, and re-layouts  10 us (13%)
    pallas_call x1, Pallas kernels, local(): pl.pallas_call(functools.partial(kernel, n_row, n_col, n_band), out_shape...  67.3 us
    unnamed x3, local copies, waits for them, and re-layouts  6.04 us
    transpose x1, local copies, waits for them, and re-layouts, local(): return jnp.transpose(out[:, :bands], (1, 0, 2))  3.96 us

profile of v1, /device:TPU:0, one launch (start us, length us, event | category | flops | bytes accessed | tf_op | source)
XLA Modules:
  0.0 77.3 jit_solution(16940651883493800662)
XLA Ops:
  0.0 0.0 copy-start
  0.0 6.0 %copy.6 = f32[56,16,1024]{2,0,1:T(8,128)} copy(f32[56,16,1024]{2,1,0:T(8,128)} %param.2) | data formatting | bytes 7340032 | tf_op args[0]
  6.0 0.0 copy-done
  6.0 67.3 %shard_map.28 = f32[16,56,1024]{2,1,0:T(8,128)S(1)} custom-call(f32[16,56,1024]{2,1,0:T(8,128)} %bitcast.5, f32[16,1024]{1,0:T(8,128)S(1)} %copy-done), custom_call_target="tpu_custom_call" | custom-call | tf_op jit(solution)/shard_map/pallas_call | solution.py:428
  73.3 4.0 %copy.4 = f32[56,16,1024]{2,1,0:T(8,128)} copy(f32[56,16,1024]{2,0,1:T(8,128)S(1)} %bitcast.4) | data formatting | bytes 7340032 | tf_op jit(solution)/shard_map/transpose | solution.py:465
Async XLA Ops:
  0.0 6.0 %copy-start = (f32[16,1024]{1,0:T(8,128)S(1)}, f32[16,1024]{1,0:T(8,128)}, u32[]{:S(2)}) copy-start(f32[16,1024]{1,0:T(8,128)} %w_ref.1) | copy-start | bytes 196612

commit v2 on v1

--- a/solution.py
+++ b/solution.py
@@ -21,7 +21,7 @@
            N, U, W, QX, QY, HU, HD, E, ER, EL, WT, SC, CY, S, SE, R, RE,
            LA, LB, FA, FB, MA, MB,
            in_sem, out_sem, ys, yr, xs, xr, zs, zr):
-    rows, bands, cols = x_ref.shape
+    bands, rows, cols = x_ref.shape
     wide = cols + LANES
     groups = bands // 8
     last = rows - 1
@@ -33,8 +33,10 @@
     has_left = ci > 0
     has_right = ci < n_col - 1
 
-    fetch = pltpu.make_async_copy(x_ref, N.at[:, 0:bands, 0:cols], in_sem)
-    fetch.start()
+    fetches = [pltpu.make_async_copy(x_ref.at[:, r, :], N.at[r, 0:bands, 0:cols], in_sem.at[r])
+               for r in range(rows)]
+    for copy in fetches:
+        copy.start()
 
     barrier = pltpu.get_barrier_semaphore()
     for cond, axis, target in ((has_up, "row", ri - 1), (has_down, "row", ri + 1),
@@ -211,7 +213,8 @@
     def _():
         EL[...] = jnp.zeros_like(EL)
 
-    fetch.wait()
+    for copy in fetches:
+        copy.wait()
     y_start(0, 0)
 
     pitch = 2 * ITERS
@@ -417,9 +420,9 @@
 def local(n_row, n_col, n_band, noisy, weight_map):
     bands, rows, cols = noisy.shape
     padded = -(-bands // 8) * 8
-    x = jnp.transpose(noisy, (1, 0, 2))
+    x = noisy
     if padded != bands:
-        x = jnp.pad(x, ((0, 0), (0, padded - bands), (0, 0)))
+        x = jnp.pad(x, ((0, padded - bands), (0, 0), (0, 0)))
     wide = cols + LANES
     f32, bf16 = jnp.float32, jnp.bfloat16
     depth = wide // LANES * (-(-padded // 16) * 16)
@@ -454,7 +457,7 @@
             pltpu.VMEM((depth, 2 * LANES), f32),
             pltpu.VMEM((2 * LANES, 2 * LANES), bf16),
             pltpu.VMEM((2 * LANES, 2 * LANES), bf16),
-            dma, dma((rows,)),
+            dma((rows,)), dma((rows,)),
             dma((2, ITERS + 1)), dma((2, ITERS + 1)),
             dma((2,)), dma((2,)),
             dma((ITERS, peers, 3)), dma((ITERS, peers, 3)),

time: 77.4 us -> 72.2 us (0.933)
  local copies, waits for them, and re-layouts: 10 us -> 4.8 us
    unnamed x3 -> x2, local copies, waits for them, and re-layouts: 6.04 us -> 0.84 us
where the time goes in v2:
time: 72.2 us; the launch traced here: 72 us
  Pallas kernels  67.2 us (93%)
  local copies, waits for them, and re-layouts  4.8 us (7%)
    pallas_call x1, Pallas kernels, local(): pl.pallas_call(functools.partial(kernel, n_row, n_col, n_band), out_shape...  67.2 us
    transpose x1, local copies, waits for them, and re-layouts, local(): return jnp.transpose(out[:, :bands], (1, 0, 2))  3.96 us

profile of v2, /device:TPU:0, one launch (start us, length us, event | category | flops | bytes accessed | tf_op | source)
XLA Modules:
  0.0 72.0 jit_solution(7743622850071990413)
XLA Ops:
  0.0 0.0 copy-start
  0.0 0.8 %copy-done = f32[16,1024]{1,0:T(8,128)S(1)} copy-done((f32[16,1024]{1,0:T(8,128)S(1)}, f32[16,1024]{1,0:T(8,128)}, u32[]{:S(2)}) %copy-start) | copy-done | bytes 65560
  0.8 67.2 %shard_map.28 = f32[16,56,1024]{2,1,0:T(8,128)S(1)} custom-call(f32[56,16,1024]{2,1,0:T(8,128)} %x_ref.1, f32[16,1024]{1,0:T(8,128)S(1)} %copy-done), custom_call_target="tpu_custom_call" | custom-call | tf_op jit(solution)/shard_map/pallas_call | solution.py:431
  68.0 4.0 %copy.3 = f32[56,16,1024]{2,1,0:T(8,128)} copy(f32[56,16,1024]{2,0,1:T(8,128)S(1)} %bitcast.1) | data formatting | bytes 7340032 | tf_op jit(solution)/shard_map/transpose | solution.py:468
Async XLA Ops:
  0.0 0.8 %copy-start = (f32[16,1024]{1,0:T(8,128)S(1)}, f32[16,1024]{1,0:T(8,128)}, u32[]{:S(2)}) copy-start(f32[16,1024]{1,0:T(8,128)} %w_ref.1) | copy-start | bytes 196612
